TPU v7x, 256 devices: a whole 4x4x8 slice. The times are simulated.
256 devices in a mesh: grp: 4 (over z_lo, core), sub: 64 (over x, z_hi, y).
Axes of the slice: x: 4, y: 4, z: 8 (z_hi: 4, z_lo: 2; z = z_hi * 2 + z_lo), core: 2. Of those that a mesh axis runs over, the one named last changes fastest.
Arguments:
- snapshots: bfloat16 [2048, 2, 256, 128], P(None, None, ('grp', 'sub')), may hold values from -6 to 6
- steering: bfloat16 [256, 2, 128, 64], P(('grp', 'sub')), may hold values from -0.375 to 0.375
- combining: bfloat16 [256, 2, 64, 1024], P(('grp', 'sub')), may hold values from -0.03125 to 0.03125
- beam_list: int32 [1024], replicated, may hold values from 0 to 1023, each once
Outputs:
- beams_out: bfloat16 [2, 2048, 1024], P(None, ('grp', 'sub'))
Inputs may be any that keep to these rules, and one draw needn't show every extreme that they name: `beam_list`: each of the 1024 beams appears once.
All inputs are finite; a program needn't handle non-finite values.
Results may differ from a plain program's by a relative error of at most 0.0065.
Values may be sent and summed in bfloat16 or wider, within the bound.
A program may use at most 128 MiB of HBM per device.

v0:
```python
import jax
import jax.numpy as jnp
from jax import lax
from jax.sharding import PartitionSpec as P


def laid_out(pieces, dim):
    lengths = list(pieces.shape[1:])
    lengths[dim] *= pieces.shape[0]
    return jnp.moveaxis(pieces, 0, dim).reshape(lengths)


def copy_for_each(shard, axis):
    size = lax.axis_size(axis)
    return lax.all_to_all(
        jnp.broadcast_to(shard[None], (size, *shard.shape)), axis, 0, 0, tiled=True
    )


def gather_directly(shard, axis, dim):
    return laid_out(copy_for_each(shard, axis), dim)


def split_up(shard, dim, size):
    before, after = (shard.shape[:dim], shard.shape[dim + 1 :])
    return jnp.moveaxis(shard.reshape(*before, size, -1, *after), dim, 0)


def sum_at_owner(shard, axis, dim):
    size = lax.axis_size(axis)
    pieces = lax.all_to_all(split_up(shard, dim, size), axis, 0, 0, tiled=True)
    return jnp.sum(pieces.astype(jnp.float32), axis=0)


def widen_block(portion):
    real_part = portion[:, 0]
    imag_part = portion[:, 1]
    top_rows = jnp.concatenate([real_part, imag_part], axis=-1)
    low_rows = jnp.concatenate([-imag_part, real_part], axis=-1)
    stacked = jnp.stack([top_rows, low_rows], axis=1)
    return stacked.reshape(portion.shape[0], 2 * portion.shape[2], 2 * portion.shape[3])


def shards(snapshots, steering, combining, beam_list):
    group_count = lax.axis_size("grp")
    sub_count = lax.axis_size("sub")
    snap_count = snapshots.shape[0]
    block_rows = snap_count // (group_count * sub_count)
    beam_count = combining.shape[3]
    sig_real = snapshots[:, 0, 0, :]
    sig_imag = snapshots[:, 1, 0, :]
    steer_real = steering[0, 0]
    steer_imag = steering[0, 1]
    upper_w = jnp.concatenate([steer_real, steer_imag], axis=1)
    lower_w = jnp.concatenate([-steer_imag, steer_real], axis=1)
    partial_value = (
        jnp.dot(sig_real, upper_w, preferred_element_type=jnp.float32)
        + jnp.dot(sig_imag, lower_w, preferred_element_type=jnp.float32)
    ).astype(jnp.bfloat16)
    ordered = jnp.take(combining, beam_list, axis=3)
    width = partial_value.shape[1]
    blocks = lax.all_to_all(
        partial_value.reshape(group_count, snap_count // group_count, width),
        "grp",
        split_axis=0,
        concat_axis=0,
        tiled=True,
    )
    gathered = gather_directly(ordered, "grp", 0)
    widened = widen_block(gathered)
    summed = sum_at_owner(
        jnp.einsum("gtc,gcn->tn", blocks, widened, preferred_element_type=jnp.float32).astype(
            jnp.bfloat16
        ),
        "sub",
        0,
    )
    shaped = summed.reshape(block_rows, 2, beam_count)
    return jnp.transpose(shaped, (1, 0, 2)).astype(jnp.bfloat16)


def solution(mesh):
    placed = (
        P(None, None, ("grp", "sub"), None),
        P(("grp", "sub"), None, None, None),
        P(("grp", "sub"), None, None, None),
        P(),
    )
    return jax.shard_map(
        shards, mesh=mesh, in_specs=placed, out_specs=P(None, ("grp", "sub"), None), check_vma=False
    )
```

profile of v0, /device:TPU:1, one launch (start us, length us, event | category | flops | bytes accessed | tf_op | source)
XLA Modules:
  0.0 110.0 jit_solution(9951625921399772056)
XLA Ops:
  0.0 0.7 fusion.11
  0.7 0.7 compare_and_fusion
  1.4 1.3 %copy.16 = bf16[1,2,64,1024]{2,1,3,0:T(2,128)(2,1)S(1)} copy(bf16[1,2,64,1024]{3,2,1,0:T(8,128)(2,1)} %param.6) | data formatting | bytes 524288 | tf_op args[2]
  2.7 3.7 %gather_fusion = bf16[1024,2,64]{2,1,0:T(2,128)(2,1)S(1)} fusion(bf16[2,64,1024]{1,0,2:T(2,128)(2,1)S(1)} %bitcast.46, s32[1024]{0:T(1024)S(1)} %fusion.11), kind=kCustom, calls=%fused_computation | custom fusion | bytes 528384 | tf_op jit(solution)/shard_map/jit(_take)/gather | solution.py:60
  6.3 3.7 %fusion.4 = bf16[2,64,1024]{1,0,2:T(2,128)(2,1)S(1)} fusion(bf16[1024,2,64]{2,1,0:T(2,128)(2,1)S(1)} %gather_fusion, pred[1024]{0:T(1024)(128)(4,1)S(1)} %compare_and_fusion), kind=kLoop, calls=%fused_computation.15 | loop fusion | flops 131072 | bytes 525312 | tf_op jit(solution)/shard_map/jit(_take)/select_n | solution.py:60
  10.1 0.0 copy-start.1
  10.1 0.0 copy-start
  10.1 0.4 copy.17
  10.5 1.1 broadcast_in_dim.21
  11.6 6.7 %all-to-all-start.1 = ((bf16[4,1,2,64,1024]{4,3,2,1,0:T(8,128)(2,1)}), bf16[4,1,2,64,1024]{4,3,2,1,0:T(8,128)(2,1)S(1)}, u32[]{:S(2)}, u32[]{:S(2)}) async-start(bf16[4,1,2,64,1024]{4,3,2,1,0:T(8,128)(2,1)} %broadcast_in_dim.21), calls=%async_computation.1 | async-start | bytes 2097152 | tf_op jit(solution)/shard_map/all_to_all | solution.py:15
  18.3 0.0 copy-done.1
  18.3 0.0 copy-done
  18.3 1.5 %fusion.16 = (bf16[2048,1,1,128]{3,1,2,0:T(2,128)(2,1)S(1)}, bf16[2048,1,1,128]{3,1,2,0:T(2,128)(2,1)S(1)}) fusion(bf16[2048,2,1,128]{3,1,2,0:T(2,128)(2,1)S(1)} %copy-done), kind=kLoop, calls=%fused_computation.31 | loop fusion | bytes 2097152 | tf_op jit(solution)/shard_map/slice | solution.py:51
  19.8 0.3 fusion.3
  20.1 0.3 fusion.2
  20.5 1.0 copy.20
  21.5 10.3 %all-to-all-done.1 = bf16[4,1,2,64,1024]{4,3,2,1,0:T(8,128)(2,1)S(1)} async-done(((bf16[4,1,2,64,1024]{4,3,2,1,0:T(8,128)(2,1)}), bf16[4,1,2,64,1024]{4,3,2,1,0:T(8,128)(2,1)S(1)}, u32[]{:S(2)}, u32[]{:S(2)}) %all-to-all-start.1) | async-done | bytes 1048608 | tf_op jit(solution)/shard_map/all_to_all | solution.py:15
  31.8 4.4 %all-to-all-start = ((bf16[4,512,128]{2,1,0:T(8,128)(2,1)}), bf16[4,512,128]{2,1,0:T(8,128)(2,1)S(1)}, u32[]{:S(2)}, u32[]{:S(2)}) async-start(bf16[4,512,128]{2,1,0:T(8,128)(2,1)} %bitcast.5), calls=%async_computation | async-start | bytes 1048576 | tf_op jit(solution)/shard_map/all_to_all | solution.py:62
  36.2 0.1 slice_bitcast_fusion
  36.3 0.2 maximum_bitcast_fusion
  36.5 0.2 pad_maximum_fusion
  36.7 0.1 copy.19
  36.8 7.2 %all-to-all-done = bf16[4,512,128]{2,1,0:T(8,128)(2,1)S(1)} async-done(((bf16[4,512,128]{2,1,0:T(8,128)(2,1)}), bf16[4,512,128]{2,1,0:T(8,128)(2,1)S(1)}, u32[]{:S(2)}, u32[]{:S(2)}) %all-to-all-start) | async-done | bytes 524320 | tf_op jit(solution)/shard_map/all_to_all | solution.py:62
  44.0 1.3 %fusion = bf16[64,8,2048]{2,1,0:T(8,128)(2,1)S(1)} fusion(bf16[4,512,128]{2,1,0:T(8,128)(2,1)S(1)} %all-to-all-done, bf16[4,128,2048]{2,1,0:T(8,128)(2,1)S(1)} %bitcast.45), kind=kOutput, calls=%fused_computation.2 | convolution fusion | flops 1074790400 | bytes 4718592 | tf_op jit(solution)/shard_map/gtc,gcn->tn/dot_general | solution.py:72
  45.3 63.8 %all_to_all.15 = bf16[64,8,2048]{2,1,0:T(8,128)(2,1)S(1)} all-to-all(bf16[64,8,2048]{2,1,0:T(8,128)(2,1)S(1)} %fusion), channel_id=1, replica_groups=mesh['grp'=4,'sub'=64] {'sub'}, dimensions={0} | all-to-all | bytes 4194304 | tf_op jit(solution)/shard_map/all_to_all | solution.py:31
  109.1 0.9 reduce_sum.12
  (3 shorter events, 0.0 us)
Async XLA Ops:
  10.1 8.2 %copy-start.1 = (bf16[1,2,128,64]{2,3,1,0:T(8,128)(2,1)S(1)}, bf16[1,2,128,64]{2,3,1,0:T(8,128)(2,1)}, u32[]{:S(2)}) copy-start(bf16[1,2,128,64]{2,3,1,0:T(8,128)(2,1)} %param.5) | copy-start | bytes 98308
  10.1 8.2 %copy-start = (bf16[2048,2,1,128]{3,1,2,0:T(2,128)(2,1)S(1)}, bf16[2048,2,1,128]{3,1,2,0:T(2,128)(2,1)}, u32[]{:S(2)}) copy-start(bf16[2048,2,1,128]{3,1,2,0:T(2,128)(2,1)} %param.4) | copy-start | bytes 3145732
  11.6 20.1 %all-to-all-start.1 = ((bf16[4,1,2,64,1024]{4,3,2,1,0:T(8,128)(2,1)}), bf16[4,1,2,64,1024]{4,3,2,1,0:T(8,128)(2,1)S(1)}, u32[]{:S(2)}, u32[]{:S(2)}) async-start(bf16[4,1,2,64,1024]{4,3,2,1,0:T(8,128)(2,1)} %broadcast_in_dim.21), calls=%async_computation.1 | async-start | bytes 2097152 | tf_op jit(solution)/shard_map/all_to_all | solution.py:15
  31.8 12.3 %all-to-all-start = ((bf16[4,512,128]{2,1,0:T(8,128)(2,1)}), bf16[4,512,128]{2,1,0:T(8,128)(2,1)S(1)}, u32[]{:S(2)}, u32[]{:S(2)}) async-start(bf16[4,512,128]{2,1,0:T(8,128)(2,1)} %bitcast.5), calls=%async_computation | async-start | bytes 1048576 | tf_op jit(solution)/shard_map/all_to_all | solution.py:62
where the time goes:
time: 112 us; the launch traced here: 110 us
  blocking collectives  63.8 us (57%)
  waiting for transfers between devices  17.5 us (16%)
  starting transfers between devices  11.1 us (10%)
  local copies, waits for them, and re-layouts  9.17 us (8%)
  other arithmetic  6.47 us (6%)
  matrix products  1.87 us (2%)
    all_to_all x1, blocking collectives, sum_at_owner(): pieces = lax.all_to_all(split_up(shard, dim, size), axis, 0, 0, tiled=True)  63.8 us
    all_to_all x1, waiting for transfers between devices, copy_for_each(): lax.all_to_all(jnp.broadcast_to(shard[None], (size, *shard.shape)), axis,...  10.3 us
    all_to_all x1, waiting for transfers between devices, shards(): lax.all_to_all(partial_value.reshape(group_count, snap_count // group_cou...  7.2 us
    all_to_all x1, starting transfers between devices, copy_for_each(): lax.all_to_all(jnp.broadcast_to(shard[None], (size, *shard.shape)), axis,...  6.68 us
    all_to_all x1, starting transfers between devices, shards(): lax.all_to_all(partial_value.reshape(group_count, snap_count // group_cou...  4.41 us
    select_n x1, other arithmetic, shards(): ordered = jnp.take(combining, beam_list, axis=3)  3.74 us
    gather x1, local copies, waits for them, and re-layouts, shards(): ordered = jnp.take(combining, beam_list, axis=3)  3.69 us
  transfers between devices with their start and end apart: 2, of which 2 were waited for; matrix products, arithmetic and copies ran while one was open for 3% of the time, Pallas kernels for 0%

commit v1 on v0

v1 whole, which is shorter than its diff:
```python
import functools

import jax
import jax.numpy as jnp
from jax import lax
from jax.experimental import pallas as pl
from jax.experimental.pallas import tpu as pltpu
from jax.sharding import PartitionSpec as P

MESH = pl.DeviceIdType.MESH
NCH = 4
BF = jnp.bfloat16
F32 = jnp.float32


def kernel(
    snap_ref, steer_ref, comb_ref, list_ref, out_ref,
    snap, steer, prod, p_send, p_all, lhs, w_all, sel, part, relay, ysum, yfin, tsum, zrecv, acc,
    load_sem, wload_sem, p_ss, p_rs, w_ss, w_rs, y_ss, y_rs, z_ss, z_rs,
):
    width = w_all.shape[-1]
    grp = lax.axis_index("grp")
    sub = lax.axis_index("sub")
    zl, core = grp // 2, grp % 2
    x, zh, y = sub // 16, (sub // 4) % 4, sub % 4
    z = zh * 2 + zl
    xp, xm, xo = (x + 1) % 4, (x + 3) % 4, (x + 2) % 4
    yp, ym, yo = (y + 1) % 4, (y + 3) % 4, (y + 2) % 4
    me = x * 2 + core

    def dev_x(x2, c2):
        return (zl * 2 + c2, x2 * 16 + zh * 4 + y)

    def dev_y(y2):
        return (grp, x * 16 + zh * 4 + y2)

    def dev_z(z2):
        return ((z2 % 2) * 2 + core, x * 16 + (z2 // 2) * 4 + y)

    def zrow(z2):
        return (z2 % 2) * 4 + z2 // 2

    loads = [
        pltpu.make_async_copy(steer_ref, steer, load_sem.at[0]),
        pltpu.make_async_copy(snap_ref, snap, load_sem.at[1]),
    ]
    for c in loads:
        c.start()
    wloads = []
    for ch in range(NCH):
        c = pltpu.make_async_copy(
            comb_ref.at[:, :, pl.ds(ch * width, width)], w_all.at[ch, me], wload_sem.at[ch]
        )
        c.start()
        wloads.append(c)

    barrier = pltpu.get_barrier_semaphore()
    peers = [dev_x((x + dx) % 4, core if dc == 0 else 1 - core)
             for dx in range(4) for dc in range(2) if dx or dc]
    peers += [dev_y(yp), dev_y(ym)]
    peers += [dev_z((z + dz) % 8) for dz in range(1, 8)]
    for p in peers:
        pl.semaphore_signal(barrier, inc=1, device_id=p, device_id_type=MESH)

    sends = []

    def remote(src, dst, ss, rs, dev):
        return pltpu.make_async_remote_copy(
            src_ref=src, dst_ref=dst, send_sem=ss, recv_sem=rs, device_id=dev, device_id_type=MESH
        )

    def send(src, dst, ss, rs, dev):
        c = remote(src, dst, ss, rs, dev)
        c.start()
        sends.append(c)

    def arrived(dst, ss, rs, dev):
        remote(dst, dst, ss, rs, dev).wait_recv()

    for c in loads:
        c.wait()
    s_re, s_im = steer[0], steer[1]
    weights = jnp.concatenate([s_re, s_im, -s_im, s_re], axis=0)
    order = [(2, 0), (2, 1), (1, 0), (1, 1), (3, 0), (3, 1), (0, 1), (0, 0)]
    for n, (dx, dc) in enumerate(order):
        x2 = (x + dx) % 4
        c2 = core if dc == 0 else 1 - core
        dest = x2 * 2 + c2
        for half in range(2):
            block = half * 8 + c2 * 4 + x2
            rows = snap[pl.ds(pl.multiple_of(block * 256, 256), 256), :]
            slot = n * 2 + half
            both = lax.dot_general(
                rows, weights, (((1,), (1,)), ((), ())), preferred_element_type=F32
            )
            prod[slot, 0] = both[:, :128]
            prod[slot, 1] = both[:, 128:]
            val = prod[slot, 0, pl.ds(0, 128, stride=2)] + prod[slot, 1, pl.ds(1, 128, stride=2)]
            for q in range(4):
                got = jnp.concatenate(
                    [val[h * 32 + q * 8 : h * 32 + q * 8 + 8] for h in range(4)], axis=0
                )
                p_send[dest, q, pl.ds(half * 32, 32), :] = got.astype(BF)

    pl.semaphore_wait(barrier, len(peers))

    def w_own(ch):
        wloads[ch].wait()
        mine = w_all.at[ch, me]
        send(mine, mine, w_ss.at[ch, 0], w_rs.at[ch, 0], dev_x(xp, core))
        send(mine, mine, w_ss.at[ch, 1], w_rs.at[ch, 1], dev_x(xm, core))
        send(mine, mine, w_ss.at[ch, 4], w_rs.at[ch, 4], dev_x(x, 1 - core))

    def p_sends():
        for dx, dc in order[:-1]:
            x2 = (x + dx) % 4
            c2 = core if dc == 0 else 1 - core
            r = dx * 2 + dc
            send(p_send.at[x2 * 2 + c2], p_all.at[me], p_ss.at[r], p_rs.at[r], dev_x(x2, c2))

    def w_relay(ch):
        a = w_all.at[ch, xm * 2 + core]
        b = w_all.at[ch, xp * 2 + core]
        arrived(a, w_ss.at[ch, 0], w_rs.at[ch, 0], dev_x(xp, core))
        send(a.at[0], a.at[0], w_ss.at[ch, 2], w_rs.at[ch, 2], dev_x(xp, core))
        send(a, a, w_ss.at[ch, 5], w_rs.at[ch, 5], dev_x(x, 1 - core))
        arrived(b, w_ss.at[ch, 1], w_rs.at[ch, 1], dev_x(xm, core))
        send(b.at[1], b.at[1], w_ss.at[ch, 3], w_rs.at[ch, 3], dev_x(xm, core))
        send(b, b, w_ss.at[ch, 6], w_rs.at[ch, 6], dev_x(x, 1 - core))

    def w_finish(ch):
        o = w_all.at[ch, xo * 2 + core]
        arrived(o.at[0], w_ss.at[ch, 2], w_rs.at[ch, 2], dev_x(xp, core))
        arrived(o.at[1], w_ss.at[ch, 3], w_rs.at[ch, 3], dev_x(xm, core))
        send(o, o, w_ss.at[ch, 7], w_rs.at[ch, 7], dev_x(x, 1 - core))
        for role, x2 in ((4, x), (5, xm), (6, xp), (7, xo)):
            arrived(
                w_all.at[ch, x2 * 2 + 1 - core], w_ss.at[ch, role], w_rs.at[ch, role],
                dev_x(x, 1 - core),
            )

    def build_lhs():
        sign = jnp.where(lax.broadcasted_iota(jnp.int32, (256, 128), 1) < 64, 1.0, -1.0)
        for dx, dc in [(0, 0)] + order[:-1]:
            x2 = (x + 4 - dx) % 4
            c2 = core if dc == 0 else 1 - core
            src = x2 * 2 + c2
            if dx or dc:
                r = dx * 2 + dc
                arrived(p_all.at[src], p_ss.at[r], p_rs.at[r], dev_x(x2, c2))
                val = p_all[src]
            else:
                val = p_send[src]
            val = val.reshape(256, 128).astype(F32)
            top = (val * sign).reshape(32, 8, 128)
            low = pltpu.roll(val, 64, 1).reshape(32, 8, 128)
            lhs[src] = jnp.concatenate([top, low], axis=1).astype(BF).reshape(512, 128)

    def multiply(ch):
        left = jnp.concatenate([lhs[k] for k in range(8)], axis=1)
        right = w_all[ch].reshape(1024, width)
        val = jnp.dot(left, right, preferred_element_type=F32)
        part[ch] = val.astype(BF).reshape(4, 8, 16, width)

    lo, hi = pl.ds(0, 4), pl.ds(4, 4)

    def y_first(ch):
        send(part.at[ch, yo, lo], relay.at[ch, 0], y_ss.at[ch, 0], y_rs.at[ch, 0], dev_y(yp))
        send(part.at[ch, yo, hi], relay.at[ch, 1], y_ss.at[ch, 1], y_rs.at[ch, 1], dev_y(ym))
        send(part.at[ch, yp, hi], yfin.at[ch, 0, hi], y_ss.at[ch, 3], y_rs.at[ch, 3], dev_y(yp))
        send(part.at[ch, ym, lo], yfin.at[ch, 1, lo], y_ss.at[ch, 4], y_rs.at[ch, 4], dev_y(ym))

    def y_relay(ch):
        arrived(relay.at[ch, 0], y_ss.at[ch, 0], y_rs.at[ch, 0], dev_y(yp))
        ysum[ch, 0] = (part[ch, yp, lo].astype(F32) + relay[ch, 0].astype(F32)).astype(BF)
        arrived(relay.at[ch, 1], y_ss.at[ch, 1], y_rs.at[ch, 1], dev_y(ym))
        ysum[ch, 1] = (part[ch, ym, hi].astype(F32) + relay[ch, 1].astype(F32)).astype(BF)
        send(ysum.at[ch, 0], yfin.at[ch, 0, lo], y_ss.at[ch, 2], y_rs.at[ch, 2], dev_y(yp))
        send(ysum.at[ch, 1], yfin.at[ch, 1, hi], y_ss.at[ch, 5], y_rs.at[ch, 5], dev_y(ym))

    def y_finish(ch):
        for role, k, rows, y2 in ((3, 0, hi, yp), (4, 1, lo, ym), (2, 0, lo, yp), (5, 1, hi, ym)):
            arrived(yfin.at[ch, k, rows], y_ss.at[ch, role], y_rs.at[ch, role], dev_y(y2))
        total = part[ch, y].astype(F32) + yfin[ch, 0].astype(F32) + yfin[ch, 1].astype(F32)
        tsum[ch] = total.astype(BF)
        for dz in (4, 3, 5, 2, 6, 1, 7):
            z2 = (z + dz) % 8
            send(tsum.at[ch, zrow(z2)], zrecv.at[ch, dz], z_ss.at[ch, dz], z_rs.at[ch, dz], dev_z(z2))

    def z_finish(ch):
        total = tsum[ch, zrow(z)].astype(F32)
        for dz in range(1, 8):
            arrived(zrecv.at[ch, dz], z_ss.at[ch, dz], z_rs.at[ch, dz], dev_z((z + dz) % 8))
        for dz in range(1, 8):
            total = total + zrecv[ch, dz].astype(F32)
        val = jnp.dot(total.astype(BF), sel[ch], preferred_element_type=F32)
        if ch == 0:
            acc[...] = val
        elif ch < NCH - 1:
            acc[...] += val
        else:
            out_ref[...] = (acc[...] + val).astype(BF)

    w_own(0)
    p_sends()
    w_own(1)
    for ch in range(NCH):
        rows = lax.broadcasted_iota(jnp.int32, (width, 1024), 0) + ch * width
        sel[ch] = jnp.where(rows == list_ref[...], 1.0, 0.0).astype(BF)
    for step in range(NCH + 2):
        if step < NCH:
            w_relay(step)
            if step + 2 < NCH:
                w_own(step + 2)
            if step == 0:
                build_lhs()
        if 1 <= step <= NCH:
            y_relay(step - 1)
        if step < NCH:
            w_finish(step)
            multiply(step)
            y_first(step)
        if 1 <= step <= NCH:
            y_finish(step - 1)
        if step >= 2:
            z_finish(step - 2)
    for c in sends:
        c.wait_send()


def solution(mesh):
    def step(snapshots, steering, combining, beam_list):
        snaps, _, _, elements = snapshots.shape
        partial = steering.shape[3]
        beams = combining.shape[3]
        width = beams // NCH
        dma = pltpu.SemaphoreType.DMA
        out = pl.pallas_call(
            kernel,
            out_shape=jax.ShapeDtypeStruct((16, beams), BF),
            in_specs=[
                pl.BlockSpec(memory_space=pl.ANY),
                pl.BlockSpec(memory_space=pl.ANY),
                pl.BlockSpec(memory_space=pl.ANY),
                pl.BlockSpec(memory_space=pltpu.VMEM),
            ],
            out_specs=pl.BlockSpec(memory_space=pltpu.VMEM),
            scratch_shapes=[
                pltpu.VMEM((2 * snaps, elements), BF),
                pltpu.VMEM((2, partial, elements), BF),
                pltpu.VMEM((16, 2, 256, 128), F32),
                pltpu.VMEM((8, 4, 64, 128), BF),
                pltpu.VMEM((8, 4, 64, 128), BF),
                pltpu.VMEM((8, 512, 128), BF),
                pltpu.VMEM((NCH, 8, 2, 64, width), BF),
                pltpu.VMEM((NCH, width, beams), BF),
                pltpu.VMEM((NCH, 4, 8, 16, width), BF),
                pltpu.VMEM((NCH, 2, 4, 16, width), BF),
                pltpu.VMEM((NCH, 2, 4, 16, width), BF),
                pltpu.VMEM((NCH, 2, 8, 16, width), BF),
                pltpu.VMEM((NCH, 8, 16, width), BF),
                pltpu.VMEM((NCH, 8, 16, width), BF),
                pltpu.VMEM((16, beams), F32),
                dma((2,)),
                dma((NCH,)),
                dma((8,)),
                dma((8,)),
                dma((NCH, 8)),
                dma((NCH, 8)),
                dma((NCH, 6)),
                dma((NCH, 6)),
                dma((NCH, 8)),
                dma((NCH, 8)),
            ],
            compiler_params=pltpu.CompilerParams(collective_id=0, has_side_effects=True),
        )(
            snapshots[:, :, 0, :].reshape(2 * snaps, elements),
            jnp.swapaxes(steering[0], 1, 2),
            combining[0],
            beam_list.reshape(1, beams),
        )
        return out.reshape(2, 8, beams)

    placed = (
        P(None, None, ("grp", "sub"), None),
        P(("grp", "sub"), None, None, None),
        P(("grp", "sub"), None, None, None),
        P(),
    )
    return jax.shard_map(
        step, mesh=mesh, in_specs=placed, out_specs=P(None, ("grp", "sub"), None), check_vma=False
    )
```

time: 112 us -> 55.4 us (0.49); the launches traced: 110 us -> 55.1 us
  blocking collectives: 63.8 us -> 0 us
  Pallas kernels: 0 us -> 53.8 us
  waiting for transfers between devices: 17.5 us -> 0 us
  starting transfers between devices: 11.1 us -> 0 us
  local copies, waits for them, and re-layouts: 9.17 us -> 1.38 us
  other arithmetic: 6.47 us -> 0 us
  matrix products: 1.87 us -> 0 us
    all_to_all x1 -> x0, blocking collectives: 63.8 us -> none  [sum_at_owner(): pieces = lax.all_to_all(split_up(shard, dim, size), axis, 0, 0, tiled=True)]
    pallas_call x0 -> x1, Pallas kernels: none -> 53.8 us  [step(): pl.pallas_call(kernel, out_shape=jax.ShapeDtypeStruct((16, beams), BF), i...]
    all_to_all x2 -> x0, waiting for transfers between devices: 17.5 us -> none  [the longest x1 10.3 us: copy_for_each(): lax.all_to_all(jnp.broadcast_to(shard[None], (size, *shard.shape)), axis,...]
    all_to_all x2 -> x0, starting transfers between devices: 11.1 us -> none  [the longest x1 6.68 us: copy_for_each(): lax.all_to_all(jnp.broadcast_to(shard[None], (size, *shard.shape)), axis,...]
    select_n x1 -> x0, other arithmetic: 3.74 us -> none  [shards(): ordered = jnp.take(combining, beam_list, axis=3)]
    gather x1 -> x0, local copies, waits for them, and re-layouts: 3.69 us -> none  [shards(): ordered = jnp.take(combining, beam_list, axis=3)]
    dot_general x3 -> x0, matrix products: 1.87 us -> none  [the longest x1 1.26 us: shards(): jnp.einsum('gtc,gcn->tn', blocks, widened, preferred_element_type=jnp.flo...]
    slice x1 -> x0, local copies, waits for them, and re-layouts: 1.5 us -> none  [shards(): sig_imag = snapshots[:, 1, 0, :]]
  transfers between devices with their start and end apart: 2 -> 0, of which waited for: 2 -> 0; matrix products, arithmetic and copies ran while one was open for 3% -> 0% of each run, Pallas kernels for 0% -> 0%
where the time goes in v1:
time: 55.4 us; the launch traced here: 55.1 us
  Pallas kernels  53.8 us (97%)
  local copies, waits for them, and re-layouts  1.38 us (2%)
    pallas_call x1, Pallas kernels, step(): pl.pallas_call(kernel, out_shape=jax.ShapeDtypeStruct((16, beams), BF), i...  53.8 us
    unnamed x1, local copies, waits for them, and re-layouts  1.38 us

profile of v1, /device:TPU:1, one launch (start us, length us, event | category | flops | bytes accessed | tf_op | source)
XLA Modules:
  0.0 55.1 jit_solution(11125582912388839330)
XLA Ops:
  0.0 53.8 %shard_map.46 = bf16[16,1024]{1,0:T(8,128)(2,1)} custom-call(bf16[4096,128]{1,0:T(8,128)(2,1)} %bitcast.7, bf16[2,64,128]{2,1,0:T(8,128)(2,1)} %bitcast.10, bf16[2,64,1024]{2,1,0:T(8,128)(2,1)} %bitcast.8, s32[1,1024]{1,0:T(1,128)} %bitcast.11), custom_call_target="tpu_custom_call" | custom-call | tf_op jit(solution)/shard_map/pallas_call | solution.py:238
  53.8 1.4 %copy.6 = bf16[2,8,1024]{2,1,0:T(8,128)(2,1)} copy(bf16[2,8,1024]{2,1,0:T(8,128)(2,1)} %bitcast.9) | data formatting | bytes 65536

commit v2 on v1

v2 whole, which is shorter than its diff:
```python
import jax
import jax.numpy as jnp
from jax import lax
from jax.experimental import pallas as pl
from jax.experimental.pallas import tpu as pltpu
from jax.sharding import PartitionSpec as P

MESH = pl.DeviceIdType.MESH
BF = jnp.bfloat16
F32 = jnp.float32
UNITS = 8
CHUNKS = ((0, 2), (2, 2), (4, 2), (6, 2))


def kernel(
    snap_ref, steer_ref, comb_ref, list_ref, out_ref,
    snap, steer, prod, p_send, p_all, lhs, w_all, sel, part, yrecv, tsum, zrecv, acc,
    load_sem, wload_sem, p_ss, p_rs, w_ss, w_rs, y_ss, y_rs, z_ss, z_rs, ring_sem,
):
    grp = lax.axis_index("grp")
    sub = lax.axis_index("sub")
    zl, core = grp // 2, grp % 2
    x, zh, y = sub // 16, (sub // 4) % 4, sub % 4
    z = zh * 2 + zl
    other = 1 - core
    me = x * 2 + core

    def dev_x(x2, c2):
        return (zl * 2 + c2, x2 * 16 + zh * 4 + y)

    def dev_y(y2):
        return (grp, x * 16 + zh * 4 + y2)

    def dev_z(z2):
        return ((z2 % 2) * 2 + core, x * 16 + (z2 // 2) * 4 + y)

    def zrow(z2):
        return (z2 % 2) * 4 + z2 // 2

    wloads = []
    for u in range(UNITS):
        c = pltpu.make_async_copy(
            comb_ref.at[:, :, pl.ds(u * 128, 128)], w_all.at[u, me], wload_sem.at[u]
        )
        wloads.append(c)
    loads = [
        pltpu.make_async_copy(steer_ref, steer, load_sem.at[0]),
        pltpu.make_async_copy(snap_ref, snap, load_sem.at[1]),
    ]
    for c in wloads[:2] + loads + wloads[2:]:
        c.start()

    barrier = pltpu.get_barrier_semaphore()
    peers = [dev_x((x + dx) % 4, core if dc == 0 else other)
             for dx in range(4) for dc in range(2) if dx or dc]
    peers += [dev_y((y + dy) % 4) for dy in range(1, 4)]
    peers += [dev_z((z + dz) % 8) for dz in (1, 7)]
    for p in peers:
        pl.semaphore_signal(barrier, inc=1, device_id=p, device_id_type=MESH)

    sends = []

    def remote(src, dst, ss, rs, dev):
        return pltpu.make_async_remote_copy(
            src_ref=src, dst_ref=dst, send_sem=ss, recv_sem=rs, device_id=dev, device_id_type=MESH
        )

    def send(src, dst, ss, rs, dev):
        c = remote(src, dst, ss, rs, dev)
        c.start()
        sends.append(c)

    def arrived(dst, ss, rs, dev):
        remote(dst, dst, ss, rs, dev).wait_recv()

    def ring_signal(k, hop):
        for j, d in enumerate((hop, 8 - hop)):
            pl.semaphore_signal(
                ring_sem.at[k, j], inc=1, device_id=dev_z((z + d) % 8), device_id_type=MESH
            )

    def ring_wait(k):
        for j in range(2):
            pl.semaphore_wait(ring_sem.at[k, j], 1)

    def w_own(ch):
        u, n = CHUNKS[ch]
        for k in range(u, u + n):
            wloads[k].wait()
        mine = w_all.at[pl.ds(u, n), me]
        for dx in (2, 1, 3):
            send(mine, mine, w_ss.at[ch, dx], w_rs.at[ch, dx], dev_x((x + dx) % 4, core))
        send(mine, mine, w_ss.at[ch, 4], w_rs.at[ch, 4], dev_x(x, other))

    def w_forward(ch):
        u, n = CHUNKS[ch]
        for dx in (1, 3, 2):
            x2 = (x + 4 - dx) % 4
            a = w_all.at[pl.ds(u, n), x2 * 2 + core]
            arrived(a, w_ss.at[ch, dx], w_rs.at[ch, dx], dev_x(x2, core))
            send(a, a, w_ss.at[ch, 4 + dx], w_rs.at[ch, 4 + dx], dev_x(x, other))

    def w_finish(ch):
        u, n = CHUNKS[ch]
        for dx in (0, 1, 3, 2):
            x2 = (x + 4 - dx) % 4
            a = w_all.at[pl.ds(u, n), x2 * 2 + other]
            arrived(a, w_ss.at[ch, 4 + dx], w_rs.at[ch, 4 + dx], dev_x(x, other))

    order = [(2, 0), (2, 1), (1, 0), (3, 0), (1, 1), (3, 1), (0, 1), (0, 0)]

    def first_section():
        for c in loads:
            c.wait()
        s_re, s_im = steer[0], steer[1]
        weights = jnp.concatenate([s_re, s_im, -s_im, s_re], axis=0)
        for n, (dx, dc) in enumerate(order):
            x2 = (x + dx) % 4
            c2 = core if dc == 0 else other
            dest = x2 * 2 + c2
            for half in range(2):
                block = half * 8 + c2 * 4 + x2
                rows = snap[pl.ds(pl.multiple_of(block * 256, 256), 256), :]
                slot = n * 2 + half
                both = lax.dot_general(
                    rows, weights, (((1,), (1,)), ((), ())), preferred_element_type=F32
                )
                prod[slot, 0] = both[:, :128]
                prod[slot, 1] = both[:, 128:]
                val = prod[slot, 0, pl.ds(0, 128, stride=2)] + prod[slot, 1, pl.ds(1, 128, stride=2)]
                for q in range(4):
                    got = jnp.concatenate(
                        [val[h * 32 + q * 8 : h * 32 + q * 8 + 8] for h in range(4)], axis=0
                    )
                    p_send[dest, q, pl.ds(half * 32, 32), :] = got.astype(BF)

    def p_sends():
        for dx, dc in order[:-1]:
            x2 = (x + dx) % 4
            c2 = core if dc == 0 else other
            r = dx * 2 + dc
            send(p_send.at[x2 * 2 + c2], p_all.at[me], p_ss.at[r], p_rs.at[r], dev_x(x2, c2))

    def build_lhs():
        sign = jnp.where(lax.broadcasted_iota(jnp.int32, (256, 128), 1) < 64, 1.0, -1.0)
        for dx, dc in [(0, 0)] + order[:-1]:
            x2 = (x + 4 - dx) % 4
            c2 = core if dc == 0 else other
            src = x2 * 2 + c2
            if dx or dc:
                r = dx * 2 + dc
                arrived(p_all.at[src], p_ss.at[r], p_rs.at[r], dev_x(x2, c2))
                val = p_all[src]
            else:
                val = p_send[src]
            val = val.reshape(256, 128).astype(F32)
            top = (val * sign).reshape(32, 8, 128)
            low = pltpu.roll(val, 64, 1).reshape(32, 8, 128)
            lhs[src] = jnp.concatenate([top, low], axis=1).astype(BF).reshape(512, 128)

    def multiply(ch):
        u, n = CHUNKS[ch]
        left = jnp.concatenate([lhs[k] for k in range(8)], axis=1)
        right = jnp.concatenate([w_all[k].reshape(1024, 128) for k in range(u, u + n)], axis=1)
        val = jnp.dot(left, right, preferred_element_type=F32)
        for k in range(n):
            part[u + k] = val[:, k * 128 : k * 128 + 128].astype(BF).reshape(4, 8, 16, 128)

    def y_send(ch):
        u, n = CHUNKS[ch]
        for dy in (2, 1, 3):
            y2 = (y + dy) % 4
            send(part.at[pl.ds(u, n), y2], yrecv.at[pl.ds(u, n), dy], y_ss.at[ch, dy], y_rs.at[ch, dy], dev_y(y2))

    def y_finish(ch):
        u, n = CHUNKS[ch]
        for dy in (1, 3, 2):
            arrived(yrecv.at[pl.ds(u, n), dy], y_ss.at[ch, dy], y_rs.at[ch, dy], dev_y((y + dy) % 4))
        for k in range(u, u + n):
            total = part[k, y].astype(F32)
            for dy in (1, 3, 2):
                total = total + yrecv[k, dy].astype(F32)
            tsum[k] = total.astype(BF)

    def z_send(ch):
        u, n = CHUNKS[ch]
        for dz in (4, 3, 5, 2, 6, 1, 7):
            z2 = (z + dz) % 8
            send(tsum.at[pl.ds(u, n), zrow(z2)], zrecv.at[pl.ds(u, n), dz], z_ss.at[ch, dz], z_rs.at[ch, dz], dev_z(z2))

    def z_finish(ch):
        u, n = CHUNKS[ch]
        for dz in range(1, 8):
            arrived(zrecv.at[pl.ds(u, n), dz], z_ss.at[ch, dz], z_rs.at[ch, dz], dev_z((z + dz) % 8))
        mine = zrow(z)
        got = []
        for k in range(u, u + n):
            total = tsum[k, mine].astype(F32)
            for dz in range(1, 8):
                total = total + zrecv[k, dz].astype(F32)
            got.append(total.astype(BF))
        val = jnp.dot(
            jnp.concatenate(got, axis=1), sel[pl.ds(u * 128, n * 128)], preferred_element_type=F32
        )
        if ch == 0:
            acc[...] = val
        elif ch < len(CHUNKS) - 1:
            acc[...] += val
        else:
            out_ref[...] = (acc[...] + val).astype(BF)

    last = len(CHUNKS)
    with jax.named_scope("barrier"):
        pl.semaphore_wait(barrier, len(peers))
    with jax.named_scope("start"):
        ring_signal(0, 1)
        w_own(0)
    with jax.named_scope("first"):
        first_section()
    with jax.named_scope("psend"):
        p_sends()
    with jax.named_scope("w_own"):
        for ch in range(1, last):
            w_own(ch)
    with jax.named_scope("sel"):
        for ch in range(UNITS // 2):
            rows = lax.broadcasted_iota(jnp.int32, (256, 1024), 0) + ch * 256
            sel[pl.ds(ch * 256, 256)] = jnp.where(rows == list_ref[...], 1.0, 0.0).astype(BF)
    with jax.named_scope("ring"):
        ring_wait(0)
        ring_signal(1, 2)
    with jax.named_scope("w_forward_0"):
        w_forward(0)
    with jax.named_scope("lhs"):
        build_lhs()
    with jax.named_scope("ringwait"):
        ring_wait(1)
    for step in range(last + 3):
        if step < last:
            if step:
                with jax.named_scope(f"w_forward_{step}"):
                    w_forward(step)
        if 2 <= step <= last + 1:
            with jax.named_scope(f"y_finish_{step-2}"):
                y_finish(step - 2)
            with jax.named_scope(f"z_send_{step-2}"):
                z_send(step - 2)
        if step < last:
            with jax.named_scope(f"w_finish_{step}"):
                w_finish(step)
            with jax.named_scope(f"mult_{step}"):
                multiply(step)
            with jax.named_scope(f"y_send_{step}"):
                y_send(step)
        if step >= 3:
            with jax.named_scope(f"z_finish_{step-3}"):
                z_finish(step - 3)
    with jax.named_scope("sends"):
        for c in sends:
            c.wait_send()


def solution(mesh):
    def step(snapshots, steering, combining, beam_list):
        snaps, _, _, elements = snapshots.shape
        partial = steering.shape[3]
        beams = combining.shape[3]
        dma = pltpu.SemaphoreType.DMA
        chunks = len(CHUNKS)
        out = pl.pallas_call(
            kernel,
            out_shape=jax.ShapeDtypeStruct((16, beams), BF),
            in_specs=[
                pl.BlockSpec(memory_space=pl.ANY),
                pl.BlockSpec(memory_space=pl.ANY),
                pl.BlockSpec(memory_space=pl.ANY),
                pl.BlockSpec(memory_space=pltpu.VMEM),
            ],
            out_specs=pl.BlockSpec(memory_space=pltpu.VMEM),
            scratch_shapes=[
                pltpu.VMEM((2 * snaps, elements), BF),
                pltpu.VMEM((2, partial, elements), BF),
                pltpu.VMEM((16, 2, 256, 128), F32),
                pltpu.VMEM((8, 4, 64, 128), BF),
                pltpu.VMEM((8, 4, 64, 128), BF),
                pltpu.VMEM((8, 512, 128), BF),
                pltpu.VMEM((UNITS, 8, 2, 64, 128), BF),
                pltpu.VMEM((beams, beams), BF),
                pltpu.VMEM((UNITS, 4, 8, 16, 128), BF),
                pltpu.VMEM((UNITS, 4, 8, 16, 128), BF),
                pltpu.VMEM((UNITS, 8, 16, 128), BF),
                pltpu.VMEM((UNITS, 8, 16, 128), BF),
                pltpu.VMEM((16, beams), F32),
                dma((2,)),
                dma((UNITS,)),
                dma((8,)),
                dma((8,)),
                dma((chunks, 8)),
                dma((chunks, 8)),
                dma((chunks, 4)),
                dma((chunks, 4)),
                dma((chunks, 8)),
                dma((chunks, 8)),
                pltpu.SemaphoreType.REGULAR((2, 2)),
            ],
            compiler_params=pltpu.CompilerParams(collective_id=0, has_side_effects=True),
        )(
            snapshots[:, :, 0, :].reshape(2 * snaps, elements),
            jnp.swapaxes(steering[0], 1, 2),
            combining[0],
            beam_list.reshape(1, beams),
        )
        return out.reshape(2, 8, beams)

    placed = (
        P(None, None, ("grp", "sub"), None),
        P(("grp", "sub"), None, None, None),
        P(("grp", "sub"), None, None, None),
        P(),
    )
    return jax.shard_map(
        step, mesh=mesh, in_specs=placed, out_specs=P(None, ("grp", "sub"), None), check_vma=False
    )
```

time: 55.4 us -> 45.5 us (0.82)
  Pallas kernels: 53.8 us -> 44 us
    pallas_call x1, Pallas kernels: 53.8 us -> 44 us  [step(): pl.pallas_call(kernel, out_shape=jax.ShapeDtypeStruct((16, beams), BF), i...]
where the time goes in v2:
time: 45.5 us; the launch traced here: 45.3 us
  Pallas kernels  44 us (97%)
  local copies, waits for them, and re-layouts  1.38 us (3%)
    pallas_call x1, Pallas kernels, step(): pl.pallas_call(kernel, out_shape=jax.ShapeDtypeStruct((16, beams), BF), i...  44 us
    unnamed x1, local copies, waits for them, and re-layouts  1.38 us

profile of v2, /device:TPU:1, one launch (start us, length us, event | category | flops | bytes accessed | tf_op | source)
XLA Modules:
  0.0 45.3 jit_solution(6282590357783545899)
XLA Ops:
  0.0 44.0 %shard_map.46 = bf16[16,1024]{1,0:T(8,128)(2,1)} custom-call(bf16[4096,128]{1,0:T(8,128)(2,1)} %bitcast.7, bf16[2,64,128]{2,1,0:T(8,128)(2,1)} %bitcast.10, bf16[2,64,1024]{2,1,0:T(8,128)(2,1)} %bitcast.8, s32[1,1024]{1,0:T(1,128)} %bitcast.11), custom_call_target="tpu_custom_call" | custom-call | tf_op jit(solution)/shard_map/pallas_call | solution.py:270
  44.0 1.4 %copy.6 = bf16[2,8,1024]{2,1,0:T(8,128)(2,1)} copy(bf16[2,8,1024]{2,1,0:T(8,128)(2,1)} %bitcast.9) | data formatting | bytes 65536

commit v3 on v2

v3 whole, which is shorter than its diff:
```python
import jax
import jax.numpy as jnp
from jax import lax
from jax.experimental import pallas as pl
from jax.experimental.pallas import tpu as pltpu
from jax.sharding import PartitionSpec as P

MESH = pl.DeviceIdType.MESH
BF = jnp.bfloat16
F32 = jnp.float32
UNITS = 8
CHUNKS = ((0, 0, 1), (1, 4, 1), (0, 1, 1), (1, 5, 1), (0, 2, 1), (1, 6, 1), (0, 3, 1), (1, 7, 1))
LAG_R = 5


def kernel(
    snap_ref, steer_ref, comb_ref, list_ref, out_ref,
    snap, steer, order_row, prod, p_send, p_all, lhs, w_all, sel, part, rrecv, tsum, zrecv, acc,
    load_sem, wload_sem, p_rs, w_rs, r_rs, z_rs, sent, ring_sem,
):
    grp = lax.axis_index("grp")
    sub = lax.axis_index("sub")
    zl, core = grp // 2, grp % 2
    x, zh, y = sub // 16, (sub // 4) % 4, sub % 4
    z = zh * 2 + zl
    other = 1 - core
    gat, red = (x, y), (y, x)
    me = (x * 2 + core, y * 2 + core)

    def dev_g(o, d, c2):
        if o == 0:
            return (zl * 2 + c2, ((x + d) % 4) * 16 + zh * 4 + y)
        return (zl * 2 + c2, x * 16 + zh * 4 + (y + d) % 4)

    def dev_r(o, d):
        return dev_g(1 - o, d, core)

    def dev_z(z2):
        return ((z2 % 2) * 2 + core, x * 16 + (z2 // 2) * 4 + y)

    def zrow(z2):
        return (z2 % 2) * 4 + z2 // 2

    owner = {}
    for o, u, n in CHUNKS:
        for k in range(u, u + n):
            owner[k] = o
    wloads = []
    for u in range(UNITS):
        c = pltpu.make_async_copy(
            comb_ref.at[:, :, pl.ds(u * 128, 128)], w_all.at[u, me[owner[u]]], wload_sem.at[u]
        )
        wloads.append(c)
    loads = [
        pltpu.make_async_copy(steer_ref, steer, load_sem.at[0]),
        pltpu.make_async_copy(snap_ref, snap, load_sem.at[1]),
        pltpu.make_async_copy(list_ref, order_row, load_sem.at[2]),
    ]
    early = [k for _, u, n in CHUNKS[:2] for k in range(u, u + n)]
    late = [k for k in range(UNITS) if k not in early]
    for c in [wloads[k] for k in early] + loads + [wloads[k] for k in late]:
        c.start()

    barrier = pltpu.get_barrier_semaphore()
    peers = [dev_g(o, d, c2) for o in range(2) for d in range(1, 4) for c2 in (core, other)]
    peers += [dev_g(0, 0, other)]
    peers += [dev_z((z + dz) % 8) for dz in (1, 7)]
    for p in peers:
        pl.semaphore_signal(barrier, inc=1, device_id=p, device_id_type=MESH)

    def send(kind, src, dst, rs, dev):
        pltpu.make_async_remote_copy(
            src_ref=src, dst_ref=dst, send_sem=sent.at[kind], recv_sem=rs, device_id=dev,
            device_id_type=MESH,
        ).start()

    def arrived(ref, rs):
        pltpu.make_async_copy(ref, ref, rs).wait()

    def ring_signal(k, hop):
        for j, d in enumerate((hop, 8 - hop)):
            pl.semaphore_signal(
                ring_sem.at[k, j], inc=1, device_id=dev_z((z + d) % 8), device_id_type=MESH
            )

    def ring_wait(k):
        for j in range(2):
            pl.semaphore_wait(ring_sem.at[k, j], 1)

    def w_own(ch):
        o, u, n = CHUNKS[ch]
        for k in range(u, u + n):
            wloads[k].wait()
        mine = w_all.at[pl.ds(u, n), me[o]]
        for d in (2, 1, 3):
            send(0, mine, mine, w_rs.at[ch, 0], dev_g(o, d, core))
        send(0, mine, mine, w_rs.at[ch, 1], dev_g(o, 0, other))

    def w_forward(ch):
        o, u, n = CHUNKS[ch]
        got = [w_all.at[pl.ds(u, n), ((gat[o] + 4 - d) % 4) * 2 + core] for d in (1, 3, 2)]
        arrived(w_all.at[pl.ds(u, n), pl.ds(0, 3)], w_rs.at[ch, 0])
        for a in got:
            send(0, a, a, w_rs.at[ch, 1], dev_g(o, 0, other))

    def w_finish(ch):
        o, u, n = CHUNKS[ch]
        arrived(w_all.at[pl.ds(u, n), pl.ds(0, 4)], w_rs.at[ch, 1])

    order = [(2, 0), (2, 1), (1, 0), (3, 0), (1, 1), (3, 1), (0, 1)]

    def first_section():
        for c in loads:
            c.wait()
        s_re, s_im = steer[0], steer[1]
        weights = jnp.concatenate([s_re, s_im, -s_im, s_re], axis=0)
        for half in range(2):
            for c2 in range(2):
                for x2 in range(4):
                    slot = half * 8 + c2 * 4 + x2
                    rows = snap[slot * 256 : slot * 256 + 256, :]
                    both = lax.dot_general(
                        rows, weights, (((1,), (1,)), ((), ())), preferred_element_type=F32
                    )
                    prod[slot, 0] = both[:, :128]
                    prod[slot, 1] = both[:, 128:]
                    val = (
                        prod[slot, 0, pl.ds(0, 128, stride=2)]
                        + prod[slot, 1, pl.ds(1, 128, stride=2)]
                    )
                    for q in range(4):
                        got = jnp.concatenate(
                            [val[h * 32 + q * 8 : h * 32 + q * 8 + 8] for h in range(4)], axis=0
                        ).astype(BF)
                        p_send[0, x2 * 2 + c2, q, half * 32 : half * 32 + 32, :] = got
                        p_send[1, q * 2 + c2, x2, half * 32 : half * 32 + 32, :] = got

    def p_sends():
        for d, dc in order:
            for o in range(2):
                c2 = core if dc == 0 else other
                dest = ((gat[o] + d) % 4) * 2 + c2
                send(1, p_send.at[o, dest], p_all.at[o, me[o]], p_rs.at[o, d], dev_g(o, d, c2))

    def build_lhs(o):
        sign = jnp.where(lax.broadcasted_iota(jnp.int32, (256, 128), 1) < 64, 1.0, -1.0)
        for d, dc in [(0, 0), (0, 1), (1, 0), (1, 1), (3, 0), (3, 1), (2, 0), (2, 1)]:
            c2 = core if dc == 0 else other
            base = ((gat[o] + 4 - d) % 4) * 2
            src = base + c2
            if d == 0 and dc:
                arrived(p_all.at[o, src], p_rs.at[o, d])
            elif d and dc == 0:
                arrived(p_all.at[o, pl.ds(base, 2)], p_rs.at[o, d])
            val = p_all[o, src] if d or dc else p_send[o, src]
            val = val.reshape(256, 128).astype(F32)
            top = (val * sign).reshape(32, 8, 128)
            low = pltpu.roll(val, 64, 1).reshape(32, 8, 128)
            lhs[o, src] = jnp.concatenate([top, low], axis=1).astype(BF).reshape(512, 128)

    def multiply(ch):
        o, u, n = CHUNKS[ch]
        left = jnp.concatenate([lhs[o, k] for k in range(8)], axis=1)
        right = jnp.concatenate([w_all[k].reshape(1024, 128) for k in range(u, u + n)], axis=1)
        val = jnp.dot(left, right, preferred_element_type=F32)
        for k in range(n):
            part[u + k] = val[:, k * 128 : k * 128 + 128].astype(BF).reshape(4, 8, 16, 128)

    def r_send(ch):
        o, u, n = CHUNKS[ch]
        for d in (2, 1, 3):
            send(
                2, part.at[pl.ds(u, n), (red[o] + d) % 4], rrecv.at[pl.ds(u, n), d],
                r_rs.at[ch], dev_r(o, d),
            )

    def r_finish(ch):
        o, u, n = CHUNKS[ch]
        arrived(rrecv.at[pl.ds(u, n), pl.ds(1, 3)], r_rs.at[ch])
        for k in range(u, u + n):
            total = part[k, red[o]].astype(F32)
            for d in (1, 3, 2):
                total = total + rrecv[k, d].astype(F32)
            tsum[k] = total.astype(BF)

    def z_send(ch):
        o, u, n = CHUNKS[ch]
        for dz in (4, 3, 5, 2, 6, 1, 7):
            z2 = (z + dz) % 8
            send(
                3, tsum.at[pl.ds(u, n), zrow(z2)], zrecv.at[pl.ds(u, n), dz],
                z_rs.at[ch], dev_z(z2),
            )

    def z_finish(ch):
        o, u, n = CHUNKS[ch]
        arrived(zrecv.at[pl.ds(u, n), pl.ds(1, 7)], z_rs.at[ch])
        mine = zrow(z)
        got = []
        for k in range(u, u + n):
            total = tsum[k, mine].astype(F32)
            for dz in range(1, 8):
                total = total + zrecv[k, dz].astype(F32)
            got.append(total.astype(BF))
        val = jnp.dot(
            jnp.concatenate(got, axis=1), sel[pl.ds(u * 128, n * 128)], preferred_element_type=F32
        )
        if ch == 0:
            acc[...] = val
        elif ch < len(CHUNKS) - 1:
            acc[...] += val
        else:
            out_ref[...] = (acc[...] + val).astype(BF)

    last = len(CHUNKS)
    scope = jax.named_scope
    with scope("barrier"):
        pl.semaphore_wait(barrier, len(peers))
    with scope("start"):
        ring_signal(0, 1)
        w_own(0)
        w_own(1)
    with scope("first"):
        first_section()
    with scope("psend"):
        p_sends()
    with scope("w_own"):
        for ch in range(2, last):
            w_own(ch)
    with scope("sel"):
        for k in range(UNITS // 2):
            rows = lax.broadcasted_iota(jnp.int32, (256, 1024), 0) + k * 256
            sel[pl.ds(k * 256, 256)] = jnp.where(rows == order_row[...], 1.0, 0.0).astype(BF)
    with scope("ring"):
        ring_wait(0)
        ring_signal(1, 2)
    with scope("w_forward_0"):
        w_forward(0)
        w_forward(1)
    with scope("lhs"):
        build_lhs(0)
        build_lhs(1)
    with scope("ringwait"):
        ring_wait(1)
    for step in range(last + LAG_R):
        if 0 < step and step + 1 < last:
            with scope(f"w_forward_{step+1}"):
                w_forward(step + 1)
        if step < last:
            with scope(f"w_finish_{step}"):
                w_finish(step)
            with scope(f"mult_{step}"):
                multiply(step)
            with scope(f"r_send_{step}"):
                r_send(step)
        if 0 <= step - LAG_R < last:
            with scope(f"r_finish_{step-LAG_R}"):
                r_finish(step - LAG_R)
            with scope(f"z_send_{step-LAG_R}"):
                z_send(step - LAG_R)
    for ch in range(last):
        with scope(f"z_finish_{ch}"):
            z_finish(ch)
    with scope("sends"):
        arrived(w_all.at[:, pl.ds(0, 7)], sent.at[0])
        arrived(p_all.at[:, pl.ds(0, 7)], sent.at[1])
        arrived(rrecv.at[:, pl.ds(0, 3)], sent.at[2])
        arrived(zrecv.at[:, pl.ds(0, 7)], sent.at[3])


def solution(mesh):
    def step(snapshots, steering, combining, beam_list):
        snaps, _, _, elements = snapshots.shape
        partial = steering.shape[3]
        beams = combining.shape[3]
        dma = pltpu.SemaphoreType.DMA
        chunks = len(CHUNKS)
        out = pl.pallas_call(
            kernel,
            out_shape=jax.ShapeDtypeStruct((16, beams), BF),
            in_specs=[
                pl.BlockSpec(memory_space=pl.ANY),
                pl.BlockSpec(memory_space=pl.ANY),
                pl.BlockSpec(memory_space=pl.ANY),
                pl.BlockSpec(memory_space=pl.ANY),
            ],
            out_specs=pl.BlockSpec(memory_space=pltpu.VMEM),
            scratch_shapes=[
                pltpu.VMEM((2 * snaps, elements), BF),
                pltpu.VMEM((2, partial, elements), BF),
                pltpu.VMEM((1, beams), jnp.int32),
                pltpu.VMEM((16, 2, 256, 128), F32),
                pltpu.VMEM((2, 8, 4, 64, 128), BF),
                pltpu.VMEM((2, 8, 4, 64, 128), BF),
                pltpu.VMEM((2, 8, 512, 128), BF),
                pltpu.VMEM((UNITS, 8, 2, 64, 128), BF),
                pltpu.VMEM((beams, beams), BF),
                pltpu.VMEM((UNITS, 4, 8, 16, 128), BF),
                pltpu.VMEM((UNITS, 4, 8, 16, 128), BF),
                pltpu.VMEM((UNITS, 8, 16, 128), BF),
                pltpu.VMEM((UNITS, 8, 16, 128), BF),
                pltpu.VMEM((16, beams), F32),
                dma((3,)),
                dma((UNITS,)),
                dma((2, 4)),
                dma((chunks, 2)),
                dma((chunks,)),
                dma((chunks,)),
                dma((4,)),
                pltpu.SemaphoreType.REGULAR((2, 2)),
            ],
            compiler_params=pltpu.CompilerParams(collective_id=0, has_side_effects=True),
        )(
            snapshots[:, :, 0, :].reshape(2 * snaps, elements),
            jnp.swapaxes(steering[0], 1, 2),
            combining[0],
            beam_list.reshape(1, beams),
        )
        return out.reshape(2, 8, beams)

    placed = (
        P(None, None, ("grp", "sub"), None),
        P(("grp", "sub"), None, None, None),
        P(("grp", "sub"), None, None, None),
        P(),
    )
    return jax.shard_map(
        step, mesh=mesh, in_specs=placed, out_specs=P(None, ("grp", "sub"), None), check_vma=False
    )
```

time: 45.5 us -> 37.7 us (0.83)
  Pallas kernels: 44 us -> 36.1 us
    pallas_call x1, Pallas kernels: 44 us -> 36.1 us  [step(): pl.pallas_call(kernel, out_shape=jax.ShapeDtypeStruct((16, beams), BF), i...]
where the time goes in v3:
time: 37.7 us; the launch traced here: 37.5 us
  Pallas kernels  36.1 us (96%)
  local copies, waits for them, and re-layouts  1.38 us (4%)
    pallas_call x1, Pallas kernels, step(): pl.pallas_call(kernel, out_shape=jax.ShapeDtypeStruct((16, beams), BF), i...  36.1 us
    unnamed x1, local copies, waits for them, and re-layouts  1.38 us

profile of v3, /device:TPU:1, one launch (start us, length us, event | category | flops | bytes accessed | tf_op | source)
XLA Modules:
  0.0 37.5 jit_solution(1937118953539017547)
XLA Ops:
  0.0 36.1 %shard_map.46 = bf16[16,1024]{1,0:T(8,128)(2,1)} custom-call(bf16[4096,128]{1,0:T(8,128)(2,1)} %bitcast.7, bf16[2,64,128]{2,1,0:T(8,128)(2,1)} %bitcast.10, bf16[2,64,1024]{2,1,0:T(8,128)(2,1)} %bitcast.8, s32[1,1024]{1,0:T(1,128)} %bitcast.11), custom_call_target="tpu_custom_call" | custom-call | tf_op jit(solution)/shard_map/pallas_call | solution.py:278
  36.1 1.4 %copy.6 = bf16[2,8,1024]{2,1,0:T(8,128)(2,1)} copy(bf16[2,8,1024]{2,1,0:T(8,128)(2,1)} %bitcast.9) | data formatting | bytes 65536

commit v4 on v3

--- a/solution.py
+++ b/solution.py
@@ -9,8 +9,7 @@
 BF = jnp.bfloat16
 F32 = jnp.float32
 UNITS = 8
-CHUNKS = ((0, 0, 1), (1, 4, 1), (0, 1, 1), (1, 5, 1), (0, 2, 1), (1, 6, 1), (0, 3, 1), (1, 7, 1))
-LAG_R = 5
+ORDER = "m0 f1 f5 m4 f2 f6 m1 m5 f3 f7 m2 m6 r0 r4 m3 m7 r1 r5 r2 r6 r3 r7"
 
 
 def kernel(
@@ -41,14 +40,10 @@
     def zrow(z2):
         return (z2 % 2) * 4 + z2 // 2
 
-    owner = {}
-    for o, u, n in CHUNKS:
-        for k in range(u, u + n):
-            owner[k] = o
     wloads = []
     for u in range(UNITS):
         c = pltpu.make_async_copy(
-            comb_ref.at[:, :, pl.ds(u * 128, 128)], w_all.at[u, me[owner[u]]], wload_sem.at[u]
+            comb_ref.at[:, :, pl.ds(u * 128, 128)], w_all.at[u, me[u // 4]], wload_sem.at[u]
         )
         wloads.append(c)
     loads = [
@@ -56,9 +51,7 @@
         pltpu.make_async_copy(snap_ref, snap, load_sem.at[1]),
         pltpu.make_async_copy(list_ref, order_row, load_sem.at[2]),
     ]
-    early = [k for _, u, n in CHUNKS[:2] for k in range(u, u + n)]
-    late = [k for k in range(UNITS) if k not in early]
-    for c in [wloads[k] for k in early] + loads + [wloads[k] for k in late]:
+    for c in [wloads[0], wloads[4]] + loads + [wloads[k] for k in (1, 5, 2, 6, 3, 7)]:
         c.start()
 
     barrier = pltpu.get_barrier_semaphore()
@@ -87,25 +80,20 @@
         for j in range(2):
             pl.semaphore_wait(ring_sem.at[k, j], 1)
 
-    def w_own(ch):
-        o, u, n = CHUNKS[ch]
-        for k in range(u, u + n):
-            wloads[k].wait()
-        mine = w_all.at[pl.ds(u, n), me[o]]
+    def w_own(u):
+        o = u // 4
+        wloads[u].wait()
+        mine = w_all.at[u, me[o]]
         for d in (2, 1, 3):
-            send(0, mine, mine, w_rs.at[ch, 0], dev_g(o, d, core))
-        send(0, mine, mine, w_rs.at[ch, 1], dev_g(o, 0, other))
-
-    def w_forward(ch):
-        o, u, n = CHUNKS[ch]
-        got = [w_all.at[pl.ds(u, n), ((gat[o] + 4 - d) % 4) * 2 + core] for d in (1, 3, 2)]
-        arrived(w_all.at[pl.ds(u, n), pl.ds(0, 3)], w_rs.at[ch, 0])
-        for a in got:
-            send(0, a, a, w_rs.at[ch, 1], dev_g(o, 0, other))
-
-    def w_finish(ch):
-        o, u, n = CHUNKS[ch]
-        arrived(w_all.at[pl.ds(u, n), pl.ds(0, 4)], w_rs.at[ch, 1])
+            send(0, mine, mine, w_rs.at[u, 0], dev_g(o, d, core))
+        send(0, mine, mine, w_rs.at[u, 1], dev_g(o, 0, other))
+
+    def w_forward(u):
+        o = u // 4
+        arrived(w_all.at[u, pl.ds(0, 3)], w_rs.at[u, 0])
+        for d in (1, 3, 2):
+            a = w_all.at[u, ((gat[o] + 4 - d) % 4) * 2 + core]
+            send(0, a, a, w_rs.at[u, 1], dev_g(o, 0, other))
 
     order = [(2, 0), (2, 1), (1, 0), (3, 0), (1, 1), (3, 1), (0, 1)]
 
@@ -158,75 +146,52 @@
             low = pltpu.roll(val, 64, 1).reshape(32, 8, 128)
             lhs[o, src] = jnp.concatenate([top, low], axis=1).astype(BF).reshape(512, 128)
 
-    def multiply(ch):
-        o, u, n = CHUNKS[ch]
+    def multiply(units):
+        o = units[0] // 4
+        for u in units:
+            arrived(w_all.at[u, pl.ds(0, 4)], w_rs.at[u, 1])
         left = jnp.concatenate([lhs[o, k] for k in range(8)], axis=1)
-        right = jnp.concatenate([w_all[k].reshape(1024, 128) for k in range(u, u + n)], axis=1)
+        right = jnp.concatenate([w_all[u].reshape(1024, 128) for u in units], axis=1)
         val = jnp.dot(left, right, preferred_element_type=F32)
-        for k in range(n):
-            part[u + k] = val[:, k * 128 : k * 128 + 128].astype(BF).reshape(4, 8, 16, 128)
-
-    def r_send(ch):
-        o, u, n = CHUNKS[ch]
-        for d in (2, 1, 3):
-            send(
-                2, part.at[pl.ds(u, n), (red[o] + d) % 4], rrecv.at[pl.ds(u, n), d],
-                r_rs.at[ch], dev_r(o, d),
-            )
-
-    def r_finish(ch):
-        o, u, n = CHUNKS[ch]
-        arrived(rrecv.at[pl.ds(u, n), pl.ds(1, 3)], r_rs.at[ch])
-        for k in range(u, u + n):
-            total = part[k, red[o]].astype(F32)
-            for d in (1, 3, 2):
-                total = total + rrecv[k, d].astype(F32)
-            tsum[k] = total.astype(BF)
-
-    def z_send(ch):
-        o, u, n = CHUNKS[ch]
+        for n, u in enumerate(units):
+            part[u] = val[:, n * 128 : n * 128 + 128].astype(BF).reshape(4, 8, 16, 128)
+        for u in units:
+            for d in (2, 1, 3):
+                send(2, part.at[u, (red[o] + d) % 4], rrecv.at[u, d], r_rs.at[u], dev_r(o, d))
+
+    def r_finish(u):
+        arrived(rrecv.at[u, pl.ds(1, 3)], r_rs.at[u])
+        total = part[u, red[u // 4]].astype(F32)
+        for d in (1, 3, 2):
+            total = total + rrecv[u, d].astype(F32)
+        tsum[u] = total.astype(BF)
         for dz in (4, 3, 5, 2, 6, 1, 7):
             z2 = (z + dz) % 8
-            send(
-                3, tsum.at[pl.ds(u, n), zrow(z2)], zrecv.at[pl.ds(u, n), dz],
-                z_rs.at[ch], dev_z(z2),
-            )
-
-    def z_finish(ch):
-        o, u, n = CHUNKS[ch]
-        arrived(zrecv.at[pl.ds(u, n), pl.ds(1, 7)], z_rs.at[ch])
-        mine = zrow(z)
-        got = []
-        for k in range(u, u + n):
-            total = tsum[k, mine].astype(F32)
-            for dz in range(1, 8):
-                total = total + zrecv[k, dz].astype(F32)
-            got.append(total.astype(BF))
-        val = jnp.dot(
-            jnp.concatenate(got, axis=1), sel[pl.ds(u * 128, n * 128)], preferred_element_type=F32
+            send(3, tsum.at[u, zrow(z2)], zrecv.at[u, dz], z_rs.at[u], dev_z(z2))
+
+    def z_finish(u):
+        arrived(zrecv.at[u, pl.ds(1, 7)], z_rs.at[u])
+        total = tsum[u, zrow(z)].astype(F32)
+        for dz in range(1, 8):
+            total = total + zrecv[u, dz].astype(F32)
+        return jnp.dot(
+            total.astype(BF), sel[pl.ds(u * 128, 128)], preferred_element_type=F32
         )
-        if ch == 0:
-            acc[...] = val
-        elif ch < len(CHUNKS) - 1:
-            acc[...] += val
-        else:
-            out_ref[...] = (acc[...] + val).astype(BF)
-
-    last = len(CHUNKS)
+
     scope = jax.named_scope
     with scope("barrier"):
         pl.semaphore_wait(barrier, len(peers))
     with scope("start"):
         ring_signal(0, 1)
         w_own(0)
-        w_own(1)
+        w_own(4)
     with scope("first"):
         first_section()
     with scope("psend"):
         p_sends()
     with scope("w_own"):
-        for ch in range(2, last):
-            w_own(ch)
+        for u in (1, 5, 2, 6, 3, 7):
+            w_own(u)
     with scope("sel"):
         for k in range(UNITS // 2):
             rows = lax.broadcasted_iota(jnp.int32, (256, 1024), 0) + k * 256
@@ -236,31 +201,32 @@
         ring_signal(1, 2)
     with scope("w_forward_0"):
         w_forward(0)
-        w_forward(1)
+        w_forward(4)
     with scope("lhs"):
         build_lhs(0)
         build_lhs(1)
     with scope("ringwait"):
         ring_wait(1)
-    for step in range(last + LAG_R):
-        if 0 < step and step + 1 < last:
-            with scope(f"w_forward_{step+1}"):
-                w_forward(step + 1)
-        if step < last:
-            with scope(f"w_finish_{step}"):
-                w_finish(step)
-            with scope(f"mult_{step}"):
-                multiply(step)
-            with scope(f"r_send_{step}"):
-                r_send(step)
-        if 0 <= step - LAG_R < last:
-            with scope(f"r_finish_{step-LAG_R}"):
-                r_finish(step - LAG_R)
-            with scope(f"z_send_{step-LAG_R}"):
-                z_send(step - LAG_R)
-    for ch in range(last):
-        with scope(f"z_finish_{ch}"):
-            z_finish(ch)
+    sums = []
+    for op in ORDER.split():
+        units = [int(k) for k in op[1:]]
+        with scope(op):
+            if op[0] == "f":
+                w_forward(units[0])
+            elif op[0] == "m":
+                multiply(units)
+            else:
+                r_finish(units[0])
+                sums.append(units[0])
+    for n, u in enumerate(sums):
+        with scope(f"z{u}"):
+            val = z_finish(u)
+            if n == 0:
+                acc[...] = val
+            elif n < UNITS - 1:
+                acc[...] += val
+            else:
+                out_ref[...] = (acc[...] + val).astype(BF)
     with scope("sends"):
         arrived(w_all.at[:, pl.ds(0, 7)], sent.at[0])
         arrived(p_all.at[:, pl.ds(0, 7)], sent.at[1])
@@ -274,10 +240,9 @@
         partial = steering.shape[3]
         beams = combining.shape[3]
         dma = pltpu.SemaphoreType.DMA
-        chunks = len(CHUNKS)
         out = pl.pallas_call(
             kernel,
-            out_shape=jax.ShapeDtypeStruct((16, beams), BF),
+            out_shape=pltpu.VMEM((16, beams), BF),
             in_specs=[
                 pl.BlockSpec(memory_space=pl.ANY),
                 pl.BlockSpec(memory_space=pl.ANY),
@@ -303,9 +268,9 @@
                 dma((3,)),
                 dma((UNITS,)),
                 dma((2, 4)),
-                dma((chunks, 2)),
-                dma((chunks,)),
-                dma((chunks,)),
+                dma((UNITS, 2)),
+                dma((UNITS,)),
+                dma((UNITS,)),
                 dma((4,)),
                 pltpu.SemaphoreType.REGULAR((2, 2)),
             ],

time: 37.7 us -> 35.1 us (0.931)
  Pallas kernels: 36.1 us -> 34.4 us
  local copies, waits for them, and re-layouts: 1.38 us -> 0.62 us
    pallas_call x1, Pallas kernels: 36.1 us -> 34.4 us  [step(): pl.pallas_call(kernel, out_shape=pltpu.VMEM((16, beams), BF), in_specs=[p...]
    unnamed x1, local copies, waits for them, and re-layouts: 1.38 us -> 0.62 us
where the time goes in v4:
time: 35.1 us; the launch traced here: 35 us
  Pallas kernels  34.4 us (98%)
  local copies, waits for them, and re-layouts  0.62 us (2%)
    pallas_call x1, Pallas kernels, step(): pl.pallas_call(kernel, out_shape=pltpu.VMEM((16, beams), BF), in_specs=[p...  34.4 us

profile of v4, /device:TPU:1, one launch (start us, length us, event | category | flops | bytes accessed | tf_op | source)
XLA Modules:
  0.0 35.0 jit_solution(17057912993843343471)
XLA Ops:
  0.0 34.4 %shard_map.46 = bf16[16,1024]{1,0:T(8,128)(2,1)S(1)} custom-call(bf16[4096,128]{1,0:T(8,128)(2,1)} %bitcast.8, bf16[2,64,128]{2,1,0:T(8,128)(2,1)} %bitcast.10, bf16[2,64,1024]{2,1,0:T(8,128)(2,1)} %bitcast.9, s32[1,1024]{1,0:T(1,128)} %bitcast.11), custom_call_target="tpu_custom_call" | custom-call | tf_op jit(solution)/shard_map/pallas_call | solution.py:243
  34.4 0.6 %copy.6 = bf16[2,8,1024]{2,1,0:T(8,128)(2,1)} copy(bf16[2,8,1024]{2,1,0:T(8,128)(2,1)S(1)} %bitcast.7) | data formatting | bytes 65536

commit v5 on v4

--- a/solution.py
+++ b/solution.py
@@ -9,12 +9,18 @@
 BF = jnp.bfloat16
 F32 = jnp.float32
 UNITS = 8
-ORDER = "m0 f1 f5 m4 f2 f6 m1 m5 f3 f7 m2 m6 r0 r4 m3 m7 r1 r5 r2 r6 r3 r7"
+BEFORE = (0, 4)
+EARLY_Z = (0, 4)
+ORDER = (
+    "m04", "f15", "m15", "f26", "f37", "m26", "m37", "r15",
+    "r26", "z04", "r37", "e1", "e5", "e2", "e6", "e0",
+    "e4", "e3", "e7",
+)
 
 
 def kernel(
     snap_ref, steer_ref, comb_ref, list_ref, out_ref,
-    snap, steer, order_row, prod, p_send, p_all, lhs, w_all, sel, part, rrecv, tsum, zrecv, acc,
+    snap, steer, order_row, prod, p_send, p_all, lhs, w_all, sel, part, rrecv, tsum, zrecv, zfirst, zsum, rlast, acc,
     load_sem, wload_sem, p_rs, w_rs, r_rs, z_rs, sent, ring_sem,
 ):
     grp = lax.axis_index("grp")
@@ -51,7 +57,7 @@
         pltpu.make_async_copy(snap_ref, snap, load_sem.at[1]),
         pltpu.make_async_copy(list_ref, order_row, load_sem.at[2]),
     ]
-    for c in [wloads[0], wloads[4]] + loads + [wloads[k] for k in (1, 5, 2, 6, 3, 7)]:
+    for c in [wloads[k] for k in (0, 4, 1, 5)] + loads + [wloads[k] for k in (2, 6, 3, 7)]:
         c.start()
 
     barrier = pltpu.get_barrier_semaphore()
@@ -84,15 +90,15 @@
         o = u // 4
         wloads[u].wait()
         mine = w_all.at[u, me[o]]
-        for d in (2, 1, 3):
+        for d in (1, 3, 2):
             send(0, mine, mine, w_rs.at[u, 0], dev_g(o, d, core))
         send(0, mine, mine, w_rs.at[u, 1], dev_g(o, 0, other))
 
     def w_forward(u):
         o = u // 4
+        got = [w_all.at[u, ((gat[o] + 4 - d) % 4) * 2 + core] for d in (1, 3, 2)]
         arrived(w_all.at[u, pl.ds(0, 3)], w_rs.at[u, 0])
-        for d in (1, 3, 2):
-            a = w_all.at[u, ((gat[o] + 4 - d) % 4) * 2 + core]
+        for a in got:
             send(0, a, a, w_rs.at[u, 1], dev_g(o, 0, other))
 
     order = [(2, 0), (2, 1), (1, 0), (3, 0), (1, 1), (3, 1), (0, 1)]
@@ -130,36 +136,43 @@
                 dest = ((gat[o] + d) % 4) * 2 + c2
                 send(1, p_send.at[o, dest], p_all.at[o, me[o]], p_rs.at[o, d], dev_g(o, d, c2))
 
-    def build_lhs(o):
-        sign = jnp.where(lax.broadcasted_iota(jnp.int32, (256, 128), 1) < 64, 1.0, -1.0)
-        for d, dc in [(0, 0), (0, 1), (1, 0), (1, 1), (3, 0), (3, 1), (2, 0), (2, 1)]:
-            c2 = core if dc == 0 else other
-            base = ((gat[o] + 4 - d) % 4) * 2
-            src = base + c2
-            if d == 0 and dc:
-                arrived(p_all.at[o, src], p_rs.at[o, d])
-            elif d and dc == 0:
-                arrived(p_all.at[o, pl.ds(base, 2)], p_rs.at[o, d])
+    def build_lhs(o, d):
+        sign = jnp.where(lax.broadcasted_iota(jnp.int32, (256, 128), 1) < 64, 1.0, -1.0).astype(BF)
+        base = ((gat[o] + 4 - d) % 4) * 2
+        if d:
+            arrived(p_all.at[o, pl.ds(base, 2)], p_rs.at[o, d])
+        else:
+            arrived(p_all.at[o, base + other], p_rs.at[o, d])
+        for dc in range(2):
+            src = base + (core if dc == 0 else other)
             val = p_all[o, src] if d or dc else p_send[o, src]
-            val = val.reshape(256, 128).astype(F32)
-            top = (val * sign).reshape(32, 8, 128)
-            low = pltpu.roll(val, 64, 1).reshape(32, 8, 128)
-            lhs[o, src] = jnp.concatenate([top, low], axis=1).astype(BF).reshape(512, 128)
+            val = val.reshape(256, 128)
+            lhs[o, src, 0:256] = val * sign
+            lhs[o, src, 256:512] = jnp.concatenate([val[:, 64:], val[:, :64]], axis=1)
 
     def multiply(units):
-        o = units[0] // 4
         for u in units:
             arrived(w_all.at[u, pl.ds(0, 4)], w_rs.at[u, 1])
-        left = jnp.concatenate([lhs[o, k] for k in range(8)], axis=1)
-        right = jnp.concatenate([w_all[u].reshape(1024, 128) for u in units], axis=1)
-        val = jnp.dot(left, right, preferred_element_type=F32)
-        for n, u in enumerate(units):
-            part[u] = val[:, n * 128 : n * 128 + 128].astype(BF).reshape(4, 8, 16, 128)
+        for o in range(2):
+            mine = [u for u in units if u // 4 == o]
+            left = jnp.concatenate([lhs[o, k] for k in range(8)], axis=1)
+            right = jnp.concatenate([w_all[u].reshape(1024, 128) for u in mine], axis=1)
+            val = jnp.dot(left, right, preferred_element_type=F32)
+            for n, u in enumerate(mine):
+                got = val[:, n * 128 : n * 128 + 128]
+                got = jnp.concatenate([got[:256].reshape(32, 8, 128), got[256:].reshape(32, 8, 128)], axis=1)
+                part[u] = got.astype(BF).reshape(4, 8, 16, 128)
         for u in units:
-            for d in (2, 1, 3):
-                send(2, part.at[u, (red[o] + d) % 4], rrecv.at[u, d], r_rs.at[u], dev_r(o, d))
-
-    def r_finish(u):
+            if u in EARLY_Z:
+                for dz in (4, 3, 5, 2, 6, 1, 7):
+                    z2 = (z + dz) % 8
+                    send(4, part.at[u, :, zrow(z2)], zfirst.at[EARLY_Z.index(u), dz], z_rs.at[u], dev_z(z2))
+            else:
+                o = u // 4
+                for d in (2, 1, 3):
+                    send(2, part.at[u, (red[o] + d) % 4], rrecv.at[u, d], r_rs.at[u], dev_r(o, d))
+
+    def r_sum(u):
         arrived(rrecv.at[u, pl.ds(1, 3)], r_rs.at[u])
         total = part[u, red[u // 4]].astype(F32)
         for d in (1, 3, 2):
@@ -169,11 +182,28 @@
             z2 = (z + dz) % 8
             send(3, tsum.at[u, zrow(z2)], zrecv.at[u, dz], z_rs.at[u], dev_z(z2))
 
-    def z_finish(u):
-        arrived(zrecv.at[u, pl.ds(1, 7)], z_rs.at[u])
-        total = tsum[u, zrow(z)].astype(F32)
+    def z_sum(u):
+        n, o = EARLY_Z.index(u), u // 4
+        arrived(zfirst.at[n, pl.ds(1, 7)], z_rs.at[u])
+        total = part[u, :, zrow(z)].astype(F32)
         for dz in range(1, 8):
-            total = total + zrecv[u, dz].astype(F32)
+            total = total + zfirst[n, dz].astype(F32)
+        zsum[n] = total.astype(BF)
+        for d in (2, 1, 3):
+            send(5, zsum.at[n, (red[o] + d) % 4], rlast.at[n, d], r_rs.at[u], dev_r(o, d))
+
+    def last_sum(u):
+        if u in EARLY_Z:
+            n = EARLY_Z.index(u)
+            arrived(rlast.at[n, pl.ds(1, 3)], r_rs.at[u])
+            total = zsum[n, red[u // 4]].astype(F32)
+            for d in range(1, 4):
+                total = total + rlast[n, d].astype(F32)
+        else:
+            arrived(zrecv.at[u, pl.ds(1, 7)], z_rs.at[u])
+            total = tsum[u, zrow(z)].astype(F32)
+            for dz in range(1, 8):
+                total = total + zrecv[u, dz].astype(F32)
         return jnp.dot(
             total.astype(BF), sel[pl.ds(u * 128, 128)], preferred_element_type=F32
         )
@@ -183,15 +213,16 @@
         pl.semaphore_wait(barrier, len(peers))
     with scope("start"):
         ring_signal(0, 1)
-        w_own(0)
-        w_own(4)
+        for u in BEFORE:
+            w_own(u)
     with scope("first"):
         first_section()
     with scope("psend"):
         p_sends()
     with scope("w_own"):
-        for u in (1, 5, 2, 6, 3, 7):
-            w_own(u)
+        for u in (0, 4, 1, 5, 2, 6, 3, 7):
+            if u not in BEFORE:
+                w_own(u)
     with scope("sel"):
         for k in range(UNITS // 2):
             rows = lax.broadcasted_iota(jnp.int32, (256, 1024), 0) + k * 256
@@ -200,38 +231,45 @@
         ring_wait(0)
         ring_signal(1, 2)
     with scope("w_forward_0"):
-        w_forward(0)
-        w_forward(4)
+        for u in BEFORE:
+            w_forward(u)
     with scope("lhs"):
-        build_lhs(0)
-        build_lhs(1)
+        for d in (0, 2, 1, 3):
+            for o in range(2):
+                build_lhs(o, d)
     with scope("ringwait"):
         ring_wait(1)
-    sums = []
-    for op in ORDER.split():
+    done = 0
+    for op in ORDER:
         units = [int(k) for k in op[1:]]
         with scope(op):
-            if op[0] == "f":
-                w_forward(units[0])
-            elif op[0] == "m":
+            if op[0] == "m":
                 multiply(units)
-            else:
-                r_finish(units[0])
-                sums.append(units[0])
-    for n, u in enumerate(sums):
-        with scope(f"z{u}"):
-            val = z_finish(u)
-            if n == 0:
-                acc[...] = val
-            elif n < UNITS - 1:
-                acc[...] += val
-            else:
-                out_ref[...] = (acc[...] + val).astype(BF)
+            for u in units:
+                if op[0] == "f":
+                    w_forward(u)
+                elif op[0] == "r":
+                    r_sum(u)
+                elif op[0] == "z":
+                    z_sum(u)
+                elif op[0] == "e":
+                    val = last_sum(u)
+                    done += 1
+                    if done == 1:
+                        acc[...] = val
+                    elif done < UNITS:
+                        acc[...] += val
+                    else:
+                        out_ref[...] = (acc[...] + val).astype(BF)
     with scope("sends"):
+        rest = UNITS - len(EARLY_Z)
         arrived(w_all.at[:, pl.ds(0, 7)], sent.at[0])
         arrived(p_all.at[:, pl.ds(0, 7)], sent.at[1])
-        arrived(rrecv.at[:, pl.ds(0, 3)], sent.at[2])
-        arrived(zrecv.at[:, pl.ds(0, 7)], sent.at[3])
+        arrived(rrecv.at[pl.ds(0, rest), pl.ds(0, 3)], sent.at[2])
+        arrived(zrecv.at[pl.ds(0, rest), pl.ds(0, 7)], sent.at[3])
+        if EARLY_Z:
+            arrived(zfirst.at[:, pl.ds(0, 7)], sent.at[4])
+            arrived(rlast.at[:, pl.ds(0, 3)], sent.at[5])
 
 
 def solution(mesh):
@@ -264,6 +302,9 @@
                 pltpu.VMEM((UNITS, 4, 8, 16, 128), BF),
                 pltpu.VMEM((UNITS, 8, 16, 128), BF),
                 pltpu.VMEM((UNITS, 8, 16, 128), BF),
+                pltpu.VMEM((max(1, len(EARLY_Z)), 8, 4, 16, 128), BF),
+                pltpu.VMEM((max(1, len(EARLY_Z)), 4, 16, 128), BF),
+                pltpu.VMEM((max(1, len(EARLY_Z)), 4, 16, 128), BF),
                 pltpu.VMEM((16, beams), F32),
                 dma((3,)),
                 dma((UNITS,)),
@@ -271,7 +312,7 @@
                 dma((UNITS, 2)),
                 dma((UNITS,)),
                 dma((UNITS,)),
-                dma((4,)),
+                dma((6,)),
                 pltpu.SemaphoreType.REGULAR((2, 2)),
             ],
             compiler_params=pltpu.CompilerParams(collective_id=0, has_side_effects=True),

time: 35.1 us -> 34.7 us (0.989)
  Pallas kernels: 34.4 us -> 34 us
    pallas_call x1, Pallas kernels: 34.4 us -> 34 us  [step(): pl.pallas_call(kernel, out_shape=pltpu.VMEM((16, beams), BF), in_specs=[p...]
where the time goes in v5:
time: 34.7 us; the launch traced here: 34.6 us
  Pallas kernels  34 us (98%)
  local copies, waits for them, and re-layouts  0.62 us (2%)
    pallas_call x1, Pallas kernels, step(): pl.pallas_call(kernel, out_shape=pltpu.VMEM((16, beams), BF), in_specs=[p...  34 us

profile of v5, /device:TPU:1, one launch (start us, length us, event | category | flops | bytes accessed | tf_op | source)
XLA Modules:
  0.0 34.6 jit_solution(6638746542959867728)
XLA Ops:
  0.0 34.0 %shard_map.46 = bf16[16,1024]{1,0:T(8,128)(2,1)S(1)} custom-call(bf16[4096,128]{1,0:T(8,128)(2,1)} %bitcast.8, bf16[2,64,128]{2,1,0:T(8,128)(2,1)} %bitcast.10, bf16[2,64,1024]{2,1,0:T(8,128)(2,1)} %bitcast.9, s32[1,1024]{1,0:T(1,128)} %bitcast.11), custom_call_target="tpu_custom_call" | custom-call | tf_op jit(solution)/shard_map/pallas_call | solution.py:281
  34.0 0.6 %copy.6 = bf16[2,8,1024]{2,1,0:T(8,128)(2,1)} copy(bf16[2,8,1024]{2,1,0:T(8,128)(2,1)S(1)} %bitcast.7) | data formatting | bytes 65536

commit v6 on v5

--- a/solution.py
+++ b/solution.py
@@ -49,7 +49,7 @@
     wloads = []
     for u in range(UNITS):
         c = pltpu.make_async_copy(
-            comb_ref.at[:, :, pl.ds(u * 128, 128)], w_all.at[u, me[u // 4]], wload_sem.at[u]
+            comb_ref.at[:, :, pl.ds(u * 128, 128)], w_all.at[u, me[u // 4]], wload_sem.at[int(u not in BEFORE)]
         )
         wloads.append(c)
     loads = [
@@ -88,7 +88,6 @@
 
     def w_own(u):
         o = u // 4
-        wloads[u].wait()
         mine = w_all.at[u, me[o]]
         for d in (1, 3, 2):
             send(0, mine, mine, w_rs.at[u, 0], dev_g(o, d, core))
@@ -213,6 +212,7 @@
         pl.semaphore_wait(barrier, len(peers))
     with scope("start"):
         ring_signal(0, 1)
+        arrived(w_all.at[pl.ds(0, len(BEFORE)), 0], wload_sem.at[0])
         for u in BEFORE:
             w_own(u)
     with scope("first"):
@@ -220,6 +220,7 @@
     with scope("psend"):
         p_sends()
     with scope("w_own"):
+        arrived(w_all.at[pl.ds(0, UNITS - len(BEFORE)), 0], wload_sem.at[1])
         for u in (0, 4, 1, 5, 2, 6, 3, 7):
             if u not in BEFORE:
                 w_own(u)
@@ -307,7 +308,7 @@
                 pltpu.VMEM((max(1, len(EARLY_Z)), 4, 16, 128), BF),
                 pltpu.VMEM((16, beams), F32),
                 dma((3,)),
-                dma((UNITS,)),
+                dma((2,)),
                 dma((2, 4)),
                 dma((UNITS, 2)),
                 dma((UNITS,)),

time: 34.7 us -> 34.6 us (level)
  no operation moved by 1% of the time
where the time goes in v6:
time: 34.6 us; the launch traced here: 34.5 us
  Pallas kernels  33.9 us (98%)
  local copies, waits for them, and re-layouts  0.62 us (2%)
    pallas_call x1, Pallas kernels, step(): pl.pallas_call(kernel, out_shape=pltpu.VMEM((16, beams), BF), in_specs=[p...  33.9 us

profile of v6, /device:TPU:1, one launch (start us, length us, event | category | flops | bytes accessed | tf_op | source)
XLA Modules:
  0.0 34.5 jit_solution(4154728360128411545)
XLA Ops:
  0.0 33.9 %shard_map.46 = bf16[16,1024]{1,0:T(8,128)(2,1)S(1)} custom-call(bf16[4096,128]{1,0:T(8,128)(2,1)} %bitcast.8, bf16[2,64,128]{2,1,0:T(8,128)(2,1)} %bitcast.10, bf16[2,64,1024]{2,1,0:T(8,128)(2,1)} %bitcast.9, s32[1,1024]{1,0:T(1,128)} %bitcast.11), custom_call_target="tpu_custom_call" | custom-call | tf_op jit(solution)/shard_map/pallas_call | solution.py:282
  33.9 0.6 %copy.6 = bf16[2,8,1024]{2,1,0:T(8,128)(2,1)} copy(bf16[2,8,1024]{2,1,0:T(8,128)(2,1)S(1)} %bitcast.7) | data formatting | bytes 65536

commit v7 on v6

--- a/solution.py
+++ b/solution.py
@@ -13,8 +13,8 @@
 EARLY_Z = (0, 4)
 ORDER = (
     "m04", "f15", "m15", "f26", "f37", "m26", "m37", "r15",
-    "r26", "z04", "r37", "e1", "e5", "e2", "e6", "e0",
-    "e4", "e3", "e7",
+    "z04", "r26", "r37", "e1", "e5", "e0", "e4", "e2",
+    "e6", "e3", "e7",
 )
 
 

time: 34.6 us -> 34.6 us (level)
  no operation moved by 1% of the time
where the time goes in v7:
time: 34.6 us; the launch traced here: 34.3 us
  Pallas kernels  33.7 us (97%)
  local copies, waits for them, and re-layouts  0.62 us (2%)
    pallas_call x1, Pallas kernels, step(): pl.pallas_call(kernel, out_shape=pltpu.VMEM((16, beams), BF), in_specs=[p...  33.7 us

profile of v7, /device:TPU:1, one launch (start us, length us, event | category | flops | bytes accessed | tf_op | source)
XLA Modules:
  0.0 34.3 jit_solution(12393549812410997209)
XLA Ops:
  0.0 33.7 %shard_map.46 = bf16[16,1024]{1,0:T(8,128)(2,1)S(1)} custom-call(bf16[4096,128]{1,0:T(8,128)(2,1)} %bitcast.8, bf16[2,64,128]{2,1,0:T(8,128)(2,1)} %bitcast.10, bf16[2,64,1024]{2,1,0:T(8,128)(2,1)} %bitcast.9, s32[1,1024]{1,0:T(1,128)} %bitcast.11), custom_call_target="tpu_custom_call" | custom-call | tf_op jit(solution)/shard_map/pallas_call | solution.py:282
  33.7 0.6 %copy.6 = bf16[2,8,1024]{2,1,0:T(8,128)(2,1)} copy(bf16[2,8,1024]{2,1,0:T(8,128)(2,1)S(1)} %bitcast.7) | data formatting | bytes 65536
